TPU v7x, 32 devices: a whole 2x2x4 slice. The times are simulated.
32 devices in a mesh: groups: 2 (over y), row: 16 (over z, x, core).
Axes of the slice: x: 2, y: 2, z: 4, core: 2. Of those that a mesh axis runs over, the one named last changes fastest.
Arguments:
- raw_samples: bfloat16 [8, 1536, 1280], P('groups', 'row'), parts along dimension 0, may hold values from -64 to 64, as said below
- partner: int32 [32, 3], P(('groups', 'row')), parts along dimension 0, may hold values from -1 to 15, as said below
- counts: int32 [32, 3], P(('groups', 'row')), parts along dimension 0, may hold values from 1 to 4
Outputs:
- correlations: bfloat16 [32, 3, 80, 80, 128], P(('groups', 'row')), parts along dimension 0
There are 2 independent parts, one for each index of `groups`. A program takes and returns all parts, laid end to end along the dimension named above; each array names one. Nothing has to cross between parts.
Inputs may be any that keep to these rules, and one draw needn't show every extreme that they name: `raw_samples`: strain values of each channel and segment at their own scale. `partner`: slot 0 of row i holds i; slots 1 to r hold i + 1 to i + r for some r of 0 to 2 with i + r < 16; the other slots hold -1. Some row has r = 2. A tile stacks its first counts segments.
All inputs are finite; a program needn't handle non-finite values.
Results may differ from a plain program's by a relative error of at most 0.0075.
Values may be sent and summed in bfloat16 or wider, within the bound.
A program may use at most 128 MiB of HBM per device.

v0:
```python
import math

import jax
import jax.numpy as jnp
from jax import lax
from jax.sharding import PartitionSpec as P

SAMPLES = 1536
BINS = 192
FIRST_BIN = 5
LAGS = 128
LAG_STEP = 4
SLOTS = 3


def from_behind(value, axis, steps):
    count = lax.axis_size(axis)
    initial, last = (max(0, -steps), min(count, count - steps))
    return lax.ppermute(value, axis, [(source, source + steps) for source in range(initial, last)])


def forward_table(length, first_bin, bin_count):
    sample_idx = jnp.arange(length, dtype=jnp.int32)[:, None]
    bin_index = first_bin + jnp.arange(bin_count, dtype=jnp.int32)[None, :]
    angles = 2.0 * math.pi / length * (sample_idx * bin_index % length).astype(jnp.float32)
    return jnp.concatenate([jnp.cos(angles), -jnp.sin(angles)], axis=1).astype(jnp.bfloat16)


def lag_table(length, first_bin, bin_count, lag_count, lag_step):
    bin_index = first_bin + jnp.arange(bin_count, dtype=jnp.int32)[:, None]
    delays = lag_step * (jnp.arange(lag_count, dtype=jnp.int32)[None, :] - lag_count // 2)
    angles = 2.0 * math.pi / length * (bin_index * delays % length).astype(jnp.float32)
    return jnp.concatenate([jnp.cos(angles), -jnp.sin(angles)], axis=0).astype(jnp.bfloat16)


def whiten(samples, dft_table):
    spectra = jnp.einsum("slc,lf->scf", samples, dft_table, preferred_element_type=jnp.float32)
    energy = 2.0 * jnp.mean(spectra * spectra, axis=-1, keepdims=True)
    return (spectra * lax.rsqrt(energy + 1e-06)).astype(jnp.bfloat16)


def tile_lags(left_block, right_block, seg_count, lag_matrix, diagonal):
    segments, block_width, doubled = left_block.shape
    bin_count = doubled // 2
    keep_mask = (jnp.arange(segments, dtype=jnp.int32) < seg_count).astype(jnp.bfloat16)
    left_block = left_block * keep_mask[:, None, None]
    left_parts = jnp.stack([left_block[..., :bin_count], left_block[..., bin_count:]], axis=1)
    right_parts = jnp.stack([right_block[..., :bin_count], right_block[..., bin_count:]], axis=1)
    turned = jnp.stack([right_block[..., bin_count:], -right_block[..., :bin_count]], axis=1)
    both_right = jnp.stack([right_parts, turned], axis=1)
    cross = jnp.einsum(
        "spaf,sqpbf->abqf", left_parts, both_right, preferred_element_type=jnp.float32
    )
    scaling = lax.rsqrt(seg_count.astype(jnp.float32))
    stacked = (cross * scaling).astype(jnp.bfloat16)
    lagged = jnp.dot(
        stacked.reshape(block_width * block_width, doubled),
        lag_matrix,
        preferred_element_type=jnp.float32,
    )
    lagged = lagged.reshape(block_width, block_width, -1) * (1.0 / math.sqrt(bin_count))
    if diagonal:
        above_diag = jnp.arange(block_width)[:, None] < jnp.arange(block_width)[None, :]
        lagged = jnp.where(above_diag[:, :, None], lagged, 0.0)
    return lagged


def on_device(raw_samples, partner, counts):
    dft_table = forward_table(SAMPLES, FIRST_BIN, BINS)
    lag_matrix = lag_table(SAMPLES, FIRST_BIN, BINS, LAGS, LAG_STEP)
    own_spectra = whiten(
        lax.all_to_all(raw_samples, "row", split_axis=2, concat_axis=1, tiled=True), dft_table
    )
    neighbours = [own_spectra]
    for offset in range(1, SLOTS):
        neighbours.append(from_behind(own_spectra, "row", -offset))
    results = []
    for offset in range(SLOTS):
        is_live = partner[0, offset] >= 0
        seg_count = counts[0, offset]
        left_block = neighbours[0]
        right_block = neighbours[offset]
        diagonal = offset == 0
        lagged = tile_lags(
            left_block, right_block, seg_count, lag_matrix, diagonal
        ) * is_live.astype(jnp.float32)
        results.append(lagged.astype(jnp.bfloat16))
    return jnp.stack(results, axis=0)[None]


def solution(mesh):
    return jax.shard_map(
        on_device,
        mesh=mesh,
        in_specs=(P("groups", "row", None), P(("groups", "row"), None), P(("groups", "row"), None)),
        out_specs=P(("groups", "row"), None, None, None, None),
        check_vma=False,
    )
```

profile of v0, /device:TPU:24, one launch (start us, length us, event | category | flops | bytes accessed | tf_op | source)
XLA Modules:
  0.0 183.2 jit_solution(11634641607319630810)
XLA Ops:
  0.0 3.4 %copy.22 = bf16[4,96,1280]{1,0,2:T(4,128)(2,1)} copy(bf16[4,96,1280]{2,1,0:T(8,128)(2,1)} %param.3) | data formatting | bytes 1966080 | tf_op args[0]
  3.4 6.0 %all-to-all-start = ((bf16[4,96,1280]{1,0,2:T(4,128)(2,1)}), bf16[4,96,1280]{1,0,2:T(4,128)(2,1)S(1)}, u32[]{:S(2)}, u32[]{:S(2)}) async-start(bf16[4,96,1280]{1,0,2:T(4,128)(2,1)} %copy.22), calls=%async_computation | async-start | bytes 2621440 | tf_op jit(solution)/shard_map/all_to_all | solution.py:72
  9.5 0.6 fusion.29
  12.0 0.6 fusion.30
  14.5 0.6 compare_convert_fusion.1
  15.2 0.7 compare_convert_fusion.2
  15.8 0.6 compare_convert_fusion
  16.4 0.5 cosine_convert_fusion.1
  16.9 7.4 %cosine_convert_fusion = (bf16[1536,192]{1,0:T(8,128)(2,1)S(1)}, bf16[1536,192]{1,0:T(8,128)(2,1)}) fusion(s32[192]{0:T(256)S(1)} %iota_add_fusion), kind=kLoop, calls=%fused_computation.17 | loop fusion | flops 3538944 | bytes 1180416 | tf_op jit(solution)/shard_map/convert.3
  24.3 12.6 %all-to-all-done = bf16[4,96,1280]{1,0,2:T(4,128)(2,1)S(1)} async-done(((bf16[4,96,1280]{1,0,2:T(4,128)(2,1)}), bf16[4,96,1280]{1,0,2:T(4,128)(2,1)S(1)}, u32[]{:S(2)}, u32[]{:S(2)}) %all-to-all-start) | async-done | bytes 983072 | tf_op jit(solution)/shard_map/all_to_all | solution.py:72
  37.0 0.2 copy.23
  37.2 0.3 copy.24
  37.5 1.5 all_to_all.16
  39.0 1.9 %fusion.14 = f32[384,320]{0,1:S(1)} fusion(bf16[1536,320]{0,1:T(8,128)(2,1)S(1)} %bitcast.121, bf16[1536,192]{1,0:T(8,128)(2,1)} %get-tuple-element.33, bf16[1536,192]{1,0:T(8,128)(2,1)S(1)} %get-tuple-element.32), kind=kOutput, calls=%fused_computation.25 | convolution fusion | flops 379846656 | bytes 2654208
  40.9 0.1 multiply_reduce_fusion
  41.0 0.1 broadcast_multiply_fusion.2
  41.2 4.0 %collective-permute-start = (bf16[4,80,384]{2,1,0:T(8,128)(2,1)S(1)}, bf16[4,80,384]{2,1,0:T(8,128)(2,1)S(1)}, u32[]{:S(2)}, u32[]{:S(2)}) collective-permute-start(bf16[4,80,384]{2,1,0:T(8,128)(2,1)S(1)} %get-tuple-element.6), channel_id=1, source_target_pairs={{1,0},{2,1},{3,2},{4,3},{5,4},{6,5},{7,6},{8,7},{9,8},{10,9},{11,1... | collective-permute-start | bytes 737288 | tf_op jit(solution)/shard_map/ppermute | solution.py:19
  45.2 4.2 %collective-permute-start.1 = (bf16[4,80,384]{2,1,0:T(8,128)(2,1)S(1)}, bf16[4,80,384]{2,1,0:T(8,128)(2,1)}, u32[]{:S(2)}, u32[]{:S(2)}) collective-permute-start(bf16[4,80,384]{2,1,0:T(8,128)(2,1)S(1)} %get-tuple-element.6), channel_id=1, source_target_pairs={{2,0},{3,1},{4,2},{5,3},{6,4},{7,5},{8,6},{9,7},{10,8},{11,9},{12,... | collective-permute-start | bytes 737288 | tf_op jit(solution)/shard_map/ppermute | solution.py:19
  49.4 0.1 broadcast_multiply_fusion.1
  49.5 0.2 slice_bitcast_fusion.1
  49.8 1.0 copy.38
  50.8 1.0 copy.36
  51.8 0.2 slice_bitcast_fusion.7
  52.0 0.2 copy.34
  52.3 0.1 maximum_bitcast_fusion.1
  52.4 0.1 pad_maximum_fusion
  52.5 0.8 copy.25
  53.3 4.9 %fusion.3 = bf16[80,80,2,192]{0,1,2,3:T(8,128)(2,1)} fusion(f32[]{:T(128)S(6)} %rsqrt.18, bf16[4,2,2,80,192]{3,0,2,1,4:T(4,128)(2,1)S(1)} %copy.25, bf16[4,2,80,192,1]{2,0,1,4,3:T(4,128)(2,1)S(1)} %copy.34), kind=kOutput, calls=%fused_computation.6 | convolution fusion | flops 44236800 | bytes 5652484 | tf_op jit(solution)/shard_map/spaf,sqpbf->abqf/dot_general | solution.py:51
  58.3 19.0 %copy.27 = bf16[80,80,2,192]{3,2,1,0:T(2,128)(2,1)} copy(bf16[80,80,2,192]{0,1,2,3:T(8,128)(2,1)} %fusion.3) | data formatting | bytes 9830400 | tf_op jit(solution)/shard_map/convert_element_type | solution.py:55
  77.2 13.8 %dot_general.29 = bf16[80,80,384]{2,1,0:T(8,128)(2,1)} reshape(bf16[80,80,2,192]{3,2,1,0:T(2,128)(2,1)} %copy.27) | data formatting | bytes 9830400 | tf_op jit(solution)/shard_map/dot_general | solution.py:56
  91.0 3.4 %fusion.13 = bf16[1,80,80,128]{3,2,1,0:T(8,128)(2,1)S(1)} fusion(f32[]{:T(128)} %bitcast.19, bf16[80,80,384]{2,1,0:T(8,128)(2,1)} %dot_general.29, pred[80,80]{1,0:T(8,128)(4,1)S(1)} %iota_compare_fusion, bf16[192,128]{1,0:T(8,128)(2,1)S(1)} %get-tuple-element.31, bf16[192,128]{1,0:T(8,128)(2,1)S(1)} %get-tuple-element.30), kind=kOutput, calls=%fused_computation.24 | convolution fusion | flops 632619008 | bytes 6658308 | tf_op jit(solution)/shard_map/dot_general | solution.py:56
  94.4 0.1 slice_bitcast_fusion.10
  94.5 0.1 maximum_bitcast_fusion.4
  94.6 0.1 pad_maximum_fusion.1
  94.7 0.7 copy.28
  95.4 1.1 slice_bitcast_fusion.9
  96.5 0.1 maximum_bitcast_fusion.7
  96.6 0.1 pad_maximum_fusion.2
  96.8 1.3 copy.31
  98.0 6.3 %fusion.4 = bf16[80,80,2,192]{0,1,2,3:T(8,128)(2,1)} fusion(f32[]{:T(128)S(6)} %rsqrt.19, bf16[4,2,2,80,192]{3,0,2,1,4:T(4,128)(2,1)S(1)} %copy.28, bf16[4,2,80,192,1]{2,0,1,4,3:T(4,128)(2,1)} %copy.36), kind=kOutput, calls=%fused_computation.7 | convolution fusion | flops 44236800 | bytes 5652484 | tf_op jit(solution)/shard_map/spaf,sqpbf->abqf/dot_general | solution.py:51
  104.4 19.0 %copy.30 = bf16[80,80,2,192]{3,2,1,0:T(2,128)(2,1)} copy(bf16[80,80,2,192]{0,1,2,3:T(8,128)(2,1)} %fusion.4) | data formatting | bytes 9830400 | tf_op jit(solution)/shard_map/convert_element_type | solution.py:55
  123.4 13.9 %dot_general.32 = bf16[80,80,384]{2,1,0:T(8,128)(2,1)} reshape(bf16[80,80,2,192]{3,2,1,0:T(2,128)(2,1)} %copy.30) | data formatting | bytes 9830400 | tf_op jit(solution)/shard_map/dot_general | solution.py:56
  137.3 4.9 %fusion.5 = bf16[80,80,2,192]{0,1,2,3:T(8,128)(2,1)} fusion(f32[]{:T(128)S(6)} %rsqrt.20, bf16[4,2,2,80,192]{3,0,2,1,4:T(4,128)(2,1)S(1)} %copy-done.1, bf16[4,2,80,192,1]{2,0,1,4,3:T(4,128)(2,1)S(1)} %copy-done.2), kind=kOutput, calls=%fused_computation.8 | convolution fusion | flops 44236800 | bytes 5652484 | tf_op jit(solution)/shard_map/spaf,sqpbf->abqf/dot_general | solution.py:51
  142.2 19.0 %copy.33 = bf16[80,80,2,192]{3,2,1,0:T(2,128)(2,1)} copy(bf16[80,80,2,192]{0,1,2,3:T(8,128)(2,1)} %fusion.5) | data formatting | bytes 9830400 | tf_op jit(solution)/shard_map/convert_element_type | solution.py:55
  161.2 13.8 %dot_general.35 = bf16[80,80,384]{2,1,0:T(8,128)(2,1)} reshape(bf16[80,80,2,192]{3,2,1,0:T(2,128)(2,1)} %copy.33) | data formatting | bytes 9830400 | tf_op jit(solution)/shard_map/dot_general | solution.py:56
  174.9 4.0 %fusion.11 = bf16[1,80,80,128]{3,2,1,0:T(8,128)(2,1)S(1)} fusion(f32[]{:T(128)} %bitcast.33, bf16[80,80,384]{2,1,0:T(8,128)(2,1)} %dot_general.32, bf16[192,128]{1,0:T(8,128)(2,1)S(1)} %get-tuple-element.31, bf16[192,128]{1,0:T(8,128)(2,1)S(1)} %get-tuple-element.30), kind=kOutput, calls=%fused_computation.22 | convolution fusion | flops 630980608 | bytes 6651908 | tf_op jit(solution)/shard_map/dot_general | solution.py:56
  178.9 1.5 fusion.12
  180.4 2.8 %maximum_bitcast_fusion = bf16[1,3,80,80,128]{4,3,2,1,0:T(8,128)(2,1)} fusion(bf16[1,80,80,128]{3,2,1,0:T(8,128)(2,1)S(1)} %fusion.12, bf16[1,80,80,128]{3,2,1,0:T(8,128)(2,1)S(1)} %fusion.11, bf16[1,80,80,128]{3,2,1,0:T(8,128)(2,1)S(1)} %fusion.13), kind=kLoop, calls=%fused_computation.9 | loop fusion | flops 4915200 | bytes 9830400 | tf_op jit(solution)/shard_map/broadcast_in_dim | solution.py:88
  (19 shorter events, 0.2 us)
Async XLA Ops:
  0.0 9.4 %copy-start.3 = (s32[1,3]{1,0:T(1,128)S(1)}, s32[1,3]{1,0:T(1,128)}, u32[]{:S(2)}) copy-start(s32[1,3]{1,0:T(1,128)} %param.4) | copy-start | bytes 40
  0.0 11.9 %copy-start.4 = (s32[1,3]{1,0:T(1,128)S(1)}, s32[1,3]{1,0:T(1,128)}, u32[]{:S(2)}) copy-start(s32[1,3]{1,0:T(1,128)} %param.5) | copy-start | bytes 40
  3.4 33.6 %all-to-all-start = ((bf16[4,96,1280]{1,0,2:T(4,128)(2,1)}), bf16[4,96,1280]{1,0,2:T(4,128)(2,1)S(1)}, u32[]{:S(2)}, u32[]{:S(2)}) async-start(bf16[4,96,1280]{1,0,2:T(4,128)(2,1)} %copy.22), calls=%async_computation | async-start | bytes 2621440 | tf_op jit(solution)/shard_map/all_to_all | solution.py:72
  41.2 53.2 %collective-permute-start = (bf16[4,80,384]{2,1,0:T(8,128)(2,1)S(1)}, bf16[4,80,384]{2,1,0:T(8,128)(2,1)S(1)}, u32[]{:S(2)}, u32[]{:S(2)}) collective-permute-start(bf16[4,80,384]{2,1,0:T(8,128)(2,1)S(1)} %get-tuple-element.6), channel_id=1, source_target_pairs={{1,0},{2,1},{3,2},{4,3},{5,4},{6,5},{7,6},{8,7},{9,8},{10,9},{11,1... | collective-permute-start | bytes 737288 | tf_op jit(solution)/shard_map/ppermute | solution.py:19
  45.2 50.2 %collective-permute-start.1 = (bf16[4,80,384]{2,1,0:T(8,128)(2,1)S(1)}, bf16[4,80,384]{2,1,0:T(8,128)(2,1)}, u32[]{:S(2)}, u32[]{:S(2)}) collective-permute-start(bf16[4,80,384]{2,1,0:T(8,128)(2,1)S(1)} %get-tuple-element.6), channel_id=1, source_target_pairs={{2,0},{3,1},{4,2},{5,3},{6,4},{7,5},{8,6},{9,7},{10,8},{11,9},{12,... | collective-permute-start | bytes 737288 | tf_op jit(solution)/shard_map/ppermute | solution.py:19
  123.4 13.9 %copy-start.1 = (bf16[4,2,2,80,192]{3,0,2,1,4:T(4,128)(2,1)S(1)}, bf16[4,2,2,80,192]{3,0,2,1,4:T(4,128)(2,1)}, u32[]{:S(2)}) copy-start(bf16[4,2,2,80,192]{3,0,2,1,4:T(4,128)(2,1)} %copy.31) | copy-start | bytes 1474564
  123.4 13.9 %copy-start.2 = (bf16[4,2,80,192,1]{2,0,1,4,3:T(4,128)(2,1)S(1)}, bf16[4,2,80,192,1]{2,0,1,4,3:T(4,128)(2,1)}, u32[]{:S(2)}) copy-start(bf16[4,2,80,192,1]{2,0,1,4,3:T(4,128)(2,1)} %copy.38) | copy-start | bytes 737284
  174.9 4.0 %copy-start = (bf16[80,80,384]{2,1,0:T(8,128)(2,1)S(1)}, bf16[80,80,384]{2,1,0:T(8,128)(2,1)}, u32[]{:S(2)}) copy-start(bf16[80,80,384]{2,1,0:T(8,128)(2,1)} %dot_general.35) | copy-start | bytes 14745604
where the time goes:
time: 186 us; the launch traced here: 183 us
  local copies, waits for them, and re-layouts  110 us (59%)
  matrix products  26.9 us (14%)
  other arithmetic  15.2 us (8%)
  starting transfers between devices  14.3 us (8%)
  waiting for transfers between devices  12.6 us (7%)
  between operations  4.14 us (2%)
    convert_element_type x3, local copies, waits for them, and re-layouts, tile_lags(): stacked = (cross * scaling).astype(jnp.bfloat16)  56.9 us
    dot_general x3, local copies, waits for them, and re-layouts, tile_lags(): jnp.dot(stacked.reshape(block_width * block_width, doubled), lag_matrix,...  41.5 us
    dot_general x3, matrix products, tile_lags(): jnp.einsum('spaf,sqpbf->abqf', left_parts, both_right, preferred_element_...  16.2 us
    all_to_all x1, waiting for transfers between devices, on_device(): lax.all_to_all(raw_samples, 'row', split_axis=2, concat_axis=1, tiled=True)  12.6 us
    dot_general x3, matrix products, tile_lags(): jnp.dot(stacked.reshape(block_width * block_width, doubled), lag_matrix,...  8.82 us
    ppermute x2, starting transfers between devices, from_behind(): lax.ppermute(value, axis, [(source, source + steps) for source in range(i...  8.22 us
    another operation x2, other arithmetic  7.89 us
    all_to_all x1, starting transfers between devices, on_device(): lax.all_to_all(raw_samples, 'row', split_axis=2, concat_axis=1, tiled=True)  6.04 us
  transfers between devices with their start and end apart: 3, of which 1 were waited for; matrix products, arithmetic and copies ran while one was open for 31% of the time, Pallas kernels for 0%

commit v1 on v0

v1 whole, which is shorter than its diff:
```python
import functools
import math

import jax
import jax.numpy as jnp
import numpy as np
from jax import lax
from jax.experimental import pallas as pl
from jax.experimental.pallas import tpu as pltpu
from jax.sharding import PartitionSpec as P

SAMPLES = 1536
BINS = 192
FIRST_BIN = 5
LAGS = 128
LAG_STEP = 4
SLOTS = 3
WIDTH = 2 * BINS
HALF = BINS - 128
ROWS_PER_STEP = 8


def bin_order():
    bins = np.concatenate([np.arange(BINS), np.arange(128, BINS), np.arange(128)])
    imag = np.arange(WIDTH) >= BINS
    return bins, imag


def angle(product):
    return np.float32(2.0 * math.pi / SAMPLES) * (product % SAMPLES).astype(np.float32)


def forward_table():
    bins, imag = bin_order()
    angles = angle(np.arange(SAMPLES)[:, None] * (FIRST_BIN + bins)[None, :])
    return jnp.asarray(np.where(imag[None, :], -np.sin(angles), np.cos(angles)).astype(np.float32)).astype(jnp.bfloat16)


def lag_tables():
    bins, imag = bin_order()
    delays = LAG_STEP * (np.arange(LAGS) - LAGS // 2)
    angles = angle(delays[:, None] * (FIRST_BIN + bins)[None, :])
    straight = np.cos(angles).astype(np.float32)
    crossed = np.where(imag[None, :], -np.sin(angles), np.sin(angles)).astype(np.float32)
    return jnp.asarray(straight).astype(jnp.bfloat16), jnp.asarray(crossed).astype(jnp.bfloat16)


def from_behind(value, axis, steps):
    count = lax.axis_size(axis)
    initial, last = (max(0, -steps), min(count, count - steps))
    return lax.ppermute(value, axis, [(source, source + steps) for source in range(initial, last)])


def whiten(samples, dft_table):
    spectra = jnp.einsum("slc,lf->scf", samples, dft_table, preferred_element_type=jnp.float32)
    energy = 2.0 * jnp.mean(spectra * spectra, axis=-1, keepdims=True)
    return (spectra * lax.rsqrt(energy + 1e-06)).astype(jnp.bfloat16)


def correlate_kernel(partner, counts, own, near, far, t1, t2, out, right, rows, swapped, w0, w1):
    segments, block, width = own.shape
    step = pl.program_id(0)

    @pl.when(step == 0)
    def _():
        for slot, source in enumerate((own, near, far)):
            seg_count = counts[0, slot]
            for s in range(segments):
                keep = (s < seg_count).astype(jnp.float32)
                right[slot * block:(slot + 1) * block, s * width:(s + 1) * width] = (
                    source[s].astype(jnp.float32) * keep).astype(jnp.bfloat16)
        for s in range(segments):
            value = own[s].astype(jnp.float32)
            rows[s] = value
            swapped[s, :, 0:128] = value[:, 256:384]
            swapped[s, :, 256:384] = value[:, 0:128]
            swapped[s, :, 128:256] = pltpu.roll(value[:, 128:256], HALF, 1)

    buffers = (w0, w1)
    first = pl.multiple_of(step * ROWS_PER_STEP, ROWS_PER_STEP)
    scales = []
    for slot in range(SLOTS):
        live = (partner[0, slot] >= 0).astype(jnp.float32)
        count = jnp.full((8, LAGS), counts[0, slot].astype(jnp.float32), jnp.float32)
        scales.append((lax.rsqrt(count) * (live * (1.0 / math.sqrt(BINS))))[0:1])

    def fill(pair):
        w = buffers[pair % 2]
        for s in range(segments):
            x8 = rows[s, pl.ds(first, ROWS_PER_STEP), :]
            y8 = swapped[s, pl.ds(first, ROWS_PER_STEP), :]
            for k in range(2):
                i = 2 * pair + k
                x = jnp.broadcast_to(x8[i:i + 1], (16, width)).astype(jnp.bfloat16)
                y = jnp.broadcast_to(y8[i:i + 1], (16, width)).astype(jnp.bfloat16)
                for m in range(0, LAGS, 16):
                    w[k * LAGS + m:k * LAGS + m + 16, s * width:(s + 1) * width] = (
                        x * t1[m:m + 16, :] + y * t2[m:m + 16, :])

    pairs = ROWS_PER_STEP // 2
    fill(0)
    for pair in range(pairs):
        if pair + 1 < pairs:
            fill(pair + 1)
        result = lax.dot_general(right[...], buffers[pair % 2][...], (((1,), (1,)), ((), ())),
                                 preferred_element_type=jnp.float32)
        for k in range(2):
            a = first + 2 * pair + k
            part = result[:, k * LAGS:(k + 1) * LAGS]
            for slot in range(SLOTS):
                tile = part[slot * block:(slot + 1) * block] * scales[slot]
                if slot == 0:
                    tile = jnp.where(lax.broadcasted_iota(jnp.int32, tile.shape, 0) > a, tile, 0.0)
                out[0, slot, 2 * pair + k] = tile.astype(jnp.bfloat16)


def correlate(partner, counts, own, near, far):
    segments, block, width = own.shape
    t1, t2 = lag_tables()
    whole = lambda shape: pl.BlockSpec(shape, lambda i, *_: (0,) * len(shape))
    depth = segments * width
    return pl.pallas_call(
        correlate_kernel,
        grid_spec=pltpu.PrefetchScalarGridSpec(
            num_scalar_prefetch=2,
            grid=(block // ROWS_PER_STEP,),
            in_specs=[whole(own.shape)] * 3 + [whole(t1.shape)] * 2,
            out_specs=pl.BlockSpec((1, SLOTS, ROWS_PER_STEP, block, LAGS), lambda i, *_: (0, 0, i, 0, 0)),
            scratch_shapes=[
                pltpu.VMEM((SLOTS * block, depth), jnp.bfloat16),
                pltpu.VMEM(own.shape, jnp.float32),
                pltpu.VMEM(own.shape, jnp.float32),
                pltpu.VMEM((2 * LAGS, depth), jnp.bfloat16),
                pltpu.VMEM((2 * LAGS, depth), jnp.bfloat16),
            ],
        ),
        out_shape=jax.ShapeDtypeStruct((1, SLOTS, block, block, LAGS), jnp.bfloat16),
        cost_estimate=pl.CostEstimate(flops=2 * SLOTS * block * block * LAGS * depth, bytes_accessed=6_000_000, transcendentals=0),
        name="correlate",
    )(partner, counts, own, near, far, t1, t2)


def on_device(raw_samples, partner, counts):
    own = whiten(
        lax.all_to_all(raw_samples, "row", split_axis=2, concat_axis=1, tiled=True), forward_table()
    )
    near = from_behind(own, "row", -1)
    far = from_behind(own, "row", -2)
    return correlate(partner, counts, own, near, far)


def solution(mesh):
    return jax.shard_map(
        on_device,
        mesh=mesh,
        in_specs=(P("groups", "row", None), P(("groups", "row"), None), P(("groups", "row"), None)),
        out_specs=P(("groups", "row"), None, None, None, None),
        check_vma=False,
    )
```

time: 186 us -> 78.3 us (0.42)
  the two profiles are of different devices: /device:TPU:24 before, /device:TPU:1 now
where the time goes in v1:
time: 78.3 us; the launch traced here: 78.1 us
  blocking collectives  39 us (50%)
  Pallas kernels  16.4 us (21%)
  waiting for transfers between devices  8.98 us (11%)
  local copies, waits for them, and re-layouts  8.2 us (10%)
  starting transfers between devices  3.21 us (4%)
  matrix products  1.94 us (2%)
    all_to_all x1, blocking collectives, on_device(): lax.all_to_all(raw_samples, 'row', split_axis=2, concat_axis=1, tiled=True)  39 us
    pallas_call x1, Pallas kernels, correlate(): pl.pallas_call(correlate_kernel, grid_spec=pltpu.PrefetchScalarGridSpec(n...  16.4 us
    ppermute x2, waiting for transfers between devices, from_behind(): lax.ppermute(value, axis, [(source, source + steps) for source in range(i...  8.98 us
    unnamed x7, local copies, waits for them, and re-layouts  3.53 us
    ppermute x2, starting transfers between devices, from_behind(): lax.ppermute(value, axis, [(source, source + steps) for source in range(i...  3.21 us
    dot_general x2, local copies, waits for them, and re-layouts, whiten(): jnp.einsum('slc,lf->scf', samples, dft_table, preferred_element_type=jnp....  3.11 us
    unnamed x1, matrix products  1.94 us
  transfers between devices with their start and end apart: 2, of which 2 were waited for; matrix products, arithmetic and copies ran while one was open for 0% of the time, Pallas kernels for 0%

profile of v1, /device:TPU:1, one launch (start us, length us, event | category | flops | bytes accessed | tf_op | source)
XLA Modules:
  0.0 78.1 jit_solution(10319815320352361084)
XLA Ops:
  0.0 2.8 %copy.8 = bf16[4,96,1280]{1,0,2:T(4,128)(2,1)S(1)} copy(bf16[4,96,1280]{2,1,0:T(8,128)(2,1)} %param.6) | data formatting | bytes 1966080 | tf_op args[0]
  2.8 39.0 %all_to_all.18 = bf16[4,96,1280]{1,0,2:T(4,128)(2,1)S(1)} all-to-all(bf16[4,96,1280]{1,0,2:T(4,128)(2,1)S(1)} %copy.8), channel_id=1, replica_groups=mesh['groups'=2,'row'=16] {'row'}, dimensions={2} | all-to-all | bytes 1966080 | tf_op jit(solution)/shard_map/all_to_all | solution.py:145
  41.8 1.6 %copy.9 = bf16[4,96,1280]{2,1,0:T(8,128)(2,1)S(1)} copy(bf16[4,96,1280]{1,0,2:T(4,128)(2,1)S(1)} %all_to_all.18) | data formatting | bytes 1966080 | tf_op jit(solution)/shard_map/all_to_all | solution.py:145
  43.4 2.4 %reshape.8 = bf16[4,1536,80]{2,1,0:T(8,128)(2,1)S(1)} reshape(bf16[4,96,1280]{2,1,0:T(8,128)(2,1)S(1)} %copy.9) | data formatting | bytes 1966080 | tf_op jit(solution)/shard_map/slc,lf->scf/dot_general | solution.py:55
  45.8 0.7 copy.10
  46.5 1.9 %fusion.1 = f32[384,320]{0,1:S(1)} fusion(bf16[1536,320]{0,1:T(8,128)(2,1)S(1)} %bitcast.10, bf16[1536,384]{1,0:T(8,128)(2,1)} %constant.25), kind=kOutput, calls=%fused_computation.4 | convolution fusion | flops 377487360 | bytes 2654208
  48.4 0.1 multiply_reduce_fusion
  48.6 0.1 fusion.own
  48.7 0.0 copy-start
  48.7 1.3 %collective-permute-start.1 = (bf16[4,80,384]{2,1,0:T(8,128)(2,1)S(1)}, bf16[4,80,384]{2,1,0:T(8,128)(2,1)S(1)}, u32[]{:S(2)}, u32[]{:S(2)}) collective-permute-start(bf16[4,80,384]{2,1,0:T(8,128)(2,1)S(1)} %fusion.own), channel_id=1, source_target_pairs={{2,0},{3,1},{4,2},{5,3},{6,4},{7,5},{8,6},{9,7},{10,8},{11,9},{12,... | collective-permute-start | bytes 737288 | tf_op jit(solution)/shard_map/ppermute | solution.py:51
  50.0 1.9 %collective-permute-start = (bf16[4,80,384]{2,1,0:T(8,128)(2,1)S(1)}, bf16[4,80,384]{2,1,0:T(8,128)(2,1)S(1)}, u32[]{:S(2)}, u32[]{:S(2)}) collective-permute-start(bf16[4,80,384]{2,1,0:T(8,128)(2,1)S(1)} %fusion.own), channel_id=1, source_target_pairs={{1,0},{2,1},{3,2},{4,3},{5,4},{6,5},{7,6},{8,7},{9,8},{10,9},{11,1... | collective-permute-start | bytes 737288 | tf_op jit(solution)/shard_map/ppermute | solution.py:51
  52.0 6.6 %collective-permute-done.1.far = bf16[4,80,384]{2,1,0:T(8,128)(2,1)S(1)} collective-permute-done((bf16[4,80,384]{2,1,0:T(8,128)(2,1)S(1)}, bf16[4,80,384]{2,1,0:T(8,128)(2,1)S(1)}, u32[]{:S(2)}, u32[]{:S(2)}) %collective-permute-start.1) | collective-permute-done | bytes 245792 | tf_op jit(solution)/shard_map/ppermute | solution.py:51
  58.6 0.0 copy-start.1
  58.6 2.4 %collective-permute-done.near = bf16[4,80,384]{2,1,0:T(8,128)(2,1)S(1)} collective-permute-done((bf16[4,80,384]{2,1,0:T(8,128)(2,1)S(1)}, bf16[4,80,384]{2,1,0:T(8,128)(2,1)S(1)}, u32[]{:S(2)}, u32[]{:S(2)}) %collective-permute-start) | collective-permute-done | bytes 245792 | tf_op jit(solution)/shard_map/ppermute | solution.py:51
  61.0 0.0 copy-done
  61.0 0.0 copy-done.1
  61.0 0.0 copy-start.2
  61.0 0.7 copy-done.2
  61.6 16.4 %correlate.1 = bf16[1,3,80,80,128]{4,3,2,1,0:T(8,128)(2,1)} custom-call(s32[1,3]{1,0:T(1,128)} %partner.1, s32[1,3]{1,0:T(1,128)} %counts.1, bf16[4,80,384]{2,1,0:T(8,128)(2,1)} %copy-done, bf16[4,80,384]{2,1,0:T(8,128)(2,1)} %copy-done.2, bf16[4,80,384]{2,1,0:T(8,128)(2,1)} %copy-done.1, bf16[128,384]{1,0:T(8,128)(2,1)} %constant.21.t1, ...), custom_call_target="tpu_custom_call" | custom-call | flops 7549747200 | bytes 6000000 | tf_op jit(solution)/shard_map/correlate/pallas_call | solution.py:122
  (1 shorter events, 0.0 us)
Async XLA Ops:
  48.7 12.2 %copy-start = (bf16[4,80,384]{2,1,0:T(8,128)(2,1)}, bf16[4,80,384]{2,1,0:T(8,128)(2,1)S(1)}, u32[]{:S(2)}) copy-start(bf16[4,80,384]{2,1,0:T(8,128)(2,1)S(1)} %fusion.own) | copy-start | bytes 737284
  48.7 9.8 %collective-permute-start.1 = (bf16[4,80,384]{2,1,0:T(8,128)(2,1)S(1)}, bf16[4,80,384]{2,1,0:T(8,128)(2,1)S(1)}, u32[]{:S(2)}, u32[]{:S(2)}) collective-permute-start(bf16[4,80,384]{2,1,0:T(8,128)(2,1)S(1)} %fusion.own), channel_id=1, source_target_pairs={{2,0},{3,1},{4,2},{5,3},{6,4},{7,5},{8,6},{9,7},{10,8},{11,9},{12,... | collective-permute-start | bytes 737288 | tf_op jit(solution)/shard_map/ppermute | solution.py:51
  50.0 10.9 %collective-permute-start = (bf16[4,80,384]{2,1,0:T(8,128)(2,1)S(1)}, bf16[4,80,384]{2,1,0:T(8,128)(2,1)S(1)}, u32[]{:S(2)}, u32[]{:S(2)}) collective-permute-start(bf16[4,80,384]{2,1,0:T(8,128)(2,1)S(1)} %fusion.own), channel_id=1, source_target_pairs={{1,0},{2,1},{3,2},{4,3},{5,4},{6,5},{7,6},{8,7},{9,8},{10,9},{11,1... | collective-permute-start | bytes 737288 | tf_op jit(solution)/shard_map/ppermute | solution.py:51
  58.6 2.4 %copy-start.1 = (bf16[4,80,384]{2,1,0:T(8,128)(2,1)}, bf16[4,80,384]{2,1,0:T(8,128)(2,1)S(1)}, u32[]{:S(2)}) copy-start(bf16[4,80,384]{2,1,0:T(8,128)(2,1)S(1)} %collective-permute-done.1.far) | copy-start | bytes 737284
  61.0 0.7 copy-start.2

commit v2 on v1

--- a/solution.py
+++ b/solution.py
@@ -18,6 +18,7 @@
 WIDTH = 2 * BINS
 HALF = BINS - 128
 ROWS_PER_STEP = 8
+MESH = pl.DeviceIdType.MESH
 
 
 def bin_order():
@@ -45,16 +46,111 @@
     return jnp.asarray(straight).astype(jnp.bfloat16), jnp.asarray(crossed).astype(jnp.bfloat16)
 
 
-def from_behind(value, axis, steps):
-    count = lax.axis_size(axis)
-    initial, last = (max(0, -steps), min(count, count - steps))
-    return lax.ppermute(value, axis, [(source, source + steps) for source in range(initial, last)])
-
-
-def whiten(samples, dft_table):
-    spectra = jnp.einsum("slc,lf->scf", samples, dft_table, preferred_element_type=jnp.float32)
+def spectra_kernel(n, segments, raw, table, own, near, far, turned, landed, acc, send_sem, recv_sem, pass_send, pass_recv):
+    me = lax.axis_index("row")
+    block = own.shape[1]
+    local = table.shape[1]
+    barrier = pltpu.get_barrier_semaphore()
+
+    def ahead(k):
+        return lax.rem(me + k, n)
+
+    @pl.loop(1, n)
+    def _(k):
+        pl.semaphore_signal(barrier, inc=1, device_id={"row": ahead(k)}, device_id_type=MESH)
+
+    @pl.loop(0, raw.shape[1] // 128)
+    def _(i):
+        part = pl.ds(pl.multiple_of(i * 128, 128), 128)
+        turned[part, :] = raw[:, part].T
+
+    pl.semaphore_wait(barrier, n - 1)
+
+    def block_copy(k):
+        target = ahead(k)
+        return pltpu.make_async_remote_copy(
+            src_ref=turned.at[pl.ds(pl.multiple_of(target * block, 16), block)],
+            dst_ref=landed.at[me],
+            send_sem=send_sem.at[k],
+            recv_sem=recv_sem.at[k],
+            device_id={"row": target},
+            device_id_type=MESH,
+        )
+
+    @pl.loop(1, n)
+    def _(k):
+        block_copy(k).start()
+
+    def transform(x, source):
+        stacked = jnp.concatenate([x[:, s * local:(s + 1) * local] for s in range(segments)], axis=0)
+        return jnp.dot(stacked, table[source], preferred_element_type=jnp.float32)
+
+    acc[...] = transform(turned[pl.ds(pl.multiple_of(me * block, 16), block), :], me)
+
+    @pl.loop(1, n)
+    def _(k):
+        block_copy(k).wait_recv()
+        source = lax.rem(me + n - k, n)
+        acc[...] += transform(landed[source], source)
+
+    spectra = acc[...]
     energy = 2.0 * jnp.mean(spectra * spectra, axis=-1, keepdims=True)
-    return (spectra * lax.rsqrt(energy + 1e-06)).astype(jnp.bfloat16)
+    white = (spectra * lax.rsqrt(energy + 1e-06)).astype(jnp.bfloat16)
+    for s in range(segments):
+        own[s] = white[s * block:(s + 1) * block]
+
+    def pass_copy(i, target, place):
+        return pltpu.make_async_remote_copy(
+            src_ref=own, dst_ref=place, send_sem=pass_send.at[i], recv_sem=pass_recv.at[i],
+            device_id={"row": target}, device_id_type=MESH,
+        )
+
+    for i, place in enumerate((near, far)):
+        @pl.when(me >= i + 1)
+        def _():
+            pass_copy(i, lax.rem(me + n - i - 1, n), place).start()
+
+        @pl.when(me + i + 1 >= n)
+        def _():
+            place[...] = jnp.zeros_like(place)
+
+    @pl.loop(1, n)
+    def _(k):
+        block_copy(k).wait_send()
+
+    for i, place in enumerate((near, far)):
+        @pl.when(me + i + 1 < n)
+        def _():
+            pass_copy(i, lax.rem(me + n - i - 1, n), place).wait_recv()
+
+        @pl.when(me >= i + 1)
+        def _():
+            pass_copy(i, lax.rem(me + n - i - 1, n), place).wait_send()
+
+
+def white_blocks(raw_samples):
+    n = lax.axis_size("row")
+    segments, local, channels = raw_samples.shape
+    block = channels // n
+    white = jax.ShapeDtypeStruct((segments, block, WIDTH), jnp.bfloat16)
+    vmem = pl.BlockSpec(memory_space=pltpu.VMEM)
+    return pl.pallas_call(
+        functools.partial(spectra_kernel, n, segments),
+        out_shape=(white,) * 3,
+        in_specs=[vmem] * 2,
+        out_specs=(vmem,) * 3,
+        scratch_shapes=[
+            pltpu.VMEM((channels, segments * local), jnp.bfloat16),
+            pltpu.VMEM((n, block, segments * local), jnp.bfloat16),
+            pltpu.VMEM((segments * block, WIDTH), jnp.float32),
+            pltpu.SemaphoreType.DMA((n,)),
+            pltpu.SemaphoreType.DMA((n,)),
+            pltpu.SemaphoreType.DMA((2,)),
+            pltpu.SemaphoreType.DMA((2,)),
+        ],
+        compiler_params=pltpu.CompilerParams(collective_id=0, has_side_effects=True, vmem_limit_bytes=24 * 2**20),
+        name="white_blocks",
+    )(raw_samples.reshape(segments * local, channels), forward_table().reshape(n, local, WIDTH))
 
 
 def correlate_kernel(partner, counts, own, near, far, t1, t2, out, right, rows, swapped, w0, w1):
@@ -117,14 +213,14 @@
 def correlate(partner, counts, own, near, far):
     segments, block, width = own.shape
     t1, t2 = lag_tables()
-    whole = lambda shape: pl.BlockSpec(shape, lambda i, *_: (0,) * len(shape))
+    vmem = pl.BlockSpec(memory_space=pltpu.VMEM)
     depth = segments * width
     return pl.pallas_call(
         correlate_kernel,
         grid_spec=pltpu.PrefetchScalarGridSpec(
             num_scalar_prefetch=2,
             grid=(block // ROWS_PER_STEP,),
-            in_specs=[whole(own.shape)] * 3 + [whole(t1.shape)] * 2,
+            in_specs=[vmem] * 5,
             out_specs=pl.BlockSpec((1, SLOTS, ROWS_PER_STEP, block, LAGS), lambda i, *_: (0, 0, i, 0, 0)),
             scratch_shapes=[
                 pltpu.VMEM((SLOTS * block, depth), jnp.bfloat16),
@@ -136,16 +232,13 @@
         ),
         out_shape=jax.ShapeDtypeStruct((1, SLOTS, block, block, LAGS), jnp.bfloat16),
         cost_estimate=pl.CostEstimate(flops=2 * SLOTS * block * block * LAGS * depth, bytes_accessed=6_000_000, transcendentals=0),
+        compiler_params=pltpu.CompilerParams(vmem_limit_bytes=20 * 2**20),
         name="correlate",
     )(partner, counts, own, near, far, t1, t2)
 
 
 def on_device(raw_samples, partner, counts):
-    own = whiten(
-        lax.all_to_all(raw_samples, "row", split_axis=2, concat_axis=1, tiled=True), forward_table()
-    )
-    near = from_behind(own, "row", -1)
-    far = from_behind(own, "row", -2)
+    own, near, far = white_blocks(raw_samples)
     return correlate(partner, counts, own, near, far)
 
 

time: 78.3 us -> 58.5 us (0.75)
  the two profiles are of different devices: /device:TPU:1 before, /device:TPU:24 now
where the time goes in v2:
time: 58.5 us; the launch traced here: 58.2 us
  Pallas kernels  52.7 us (90%)
  local copies, waits for them, and re-layouts  5.56 us (10%)
    pallas_call x1, Pallas kernels, white_blocks(): pl.pallas_call(functools.partial(spectra_kernel, n, segments), out_shape=...  37.7 us
    pallas_call x1, Pallas kernels, correlate(): pl.pallas_call(correlate_kernel, grid_spec=pltpu.PrefetchScalarGridSpec(n...  14.9 us
    unnamed x12, local copies, waits for them, and re-layouts  5.56 us

profile of v2, /device:TPU:24, one launch (start us, length us, event | category | flops | bytes accessed | tf_op | source)
XLA Modules:
  0.0 58.2 jit_solution(13250509791105104716)
XLA Ops:
  0.0 0.0 copy-start
  0.0 1.3 %copy-done = bf16[16,96,384]{2,1,0:T(8,128)(2,1)S(1)} copy-done((bf16[16,96,384]{2,1,0:T(8,128)(2,1)S(1)}, bf16[16,96,384]{2,1,0:T(8,128)(2,1)}, u32[]{:S(2)}) %copy-start) | copy-done | bytes 1179672
  1.3 0.0 copy-start.1
  1.3 1.2 %copy-done.1 = bf16[4,96,1280]{2,1,0:T(8,128)(2,1)S(1)} copy-done((bf16[4,96,1280]{2,1,0:T(8,128)(2,1)S(1)}, bf16[4,96,1280]{2,1,0:T(8,128)(2,1)}, u32[]{:S(2)}) %copy-start.1) | copy-done | bytes 983064
  2.5 37.7 %white_blocks.1 = (bf16[4,80,384]{2,1,0:T(8,128)(2,1)S(1)}, bf16[4,80,384]{2,1,0:T(8,128)(2,1)S(1)}, bf16[4,80,384]{2,1,0:T(8,128)(2,1)S(1)}) custom-call(bf16[384,1280]{1,0:T(8,128)(2,1)S(1)} %bitcast.1, bf16[16,96,384]{2,1,0:T(8,128)(2,1)S(1)} %copy-done), custom_call_target="tpu_custom_call" | custom-call | tf_op jit(solution)/shard_map/white_blocks/pallas_call | solution.py:137
  40.2 0.0 copy-start.2
  40.2 0.6 %copy-done.2 = s32[1,3]{1,0:T(1,128)S(1)} copy-done((s32[1,3]{1,0:T(1,128)S(1)}, s32[1,3]{1,0:T(1,128)}, u32[]{:S(2)}) %copy-start.2) | copy-done | bytes 36
  40.9 0.0 copy-start.3
  40.9 0.7 %copy-done.3 = s32[1,3]{1,0:T(1,128)S(1)} copy-done((s32[1,3]{1,0:T(1,128)S(1)}, s32[1,3]{1,0:T(1,128)}, u32[]{:S(2)}) %copy-start.3) | copy-done | bytes 36
  41.5 0.0 copy-start.4
  41.5 0.9 %copy-done.4 = bf16[128,384]{1,0:T(8,128)(2,1)S(1)} copy-done((bf16[128,384]{1,0:T(8,128)(2,1)S(1)}, bf16[128,384]{1,0:T(8,128)(2,1)}, u32[]{:S(2)}) %copy-start.4) | copy-done | bytes 98328
  42.4 0.0 copy-start.5
  42.4 0.9 %copy-done.5 = bf16[128,384]{1,0:T(8,128)(2,1)S(1)} copy-done((bf16[128,384]{1,0:T(8,128)(2,1)S(1)}, bf16[128,384]{1,0:T(8,128)(2,1)}, u32[]{:S(2)}) %copy-start.5) | copy-done | bytes 98328
  43.3 14.9 %correlate.1 = bf16[1,3,80,80,128]{4,3,2,1,0:T(8,128)(2,1)} custom-call(s32[1,3]{1,0:T(1,128)S(1)} %copy-done.2, s32[1,3]{1,0:T(1,128)S(1)} %copy-done.3, bf16[4,80,384]{2,1,0:T(8,128)(2,1)S(1)} %get-tuple-element.8.own, bf16[4,80,384]{2,1,0:T(8,128)(2,1)S(1)} %get-tuple-element.9.near, bf16[4,80,384]{2,1,0:T(8,128)(2,1)S(1)} %get-tuple-element.10.far, ...), custom_call_target="tpu_custom_call" | custom-call | flops 7549747200 | bytes 6000000 | tf_op jit(solution)/shard_map/correlate/pallas_call | solution.py:218
Async XLA Ops:
  0.0 1.3 %copy-start = (bf16[16,96,384]{2,1,0:T(8,128)(2,1)S(1)}, bf16[16,96,384]{2,1,0:T(8,128)(2,1)}, u32[]{:S(2)}) copy-start(bf16[16,96,384]{2,1,0:T(8,128)(2,1)} %constant.12.table) | copy-start | bytes 3538948
  1.3 1.2 %copy-start.1 = (bf16[4,96,1280]{2,1,0:T(8,128)(2,1)S(1)}, bf16[4,96,1280]{2,1,0:T(8,128)(2,1)}, u32[]{:S(2)}) copy-start(bf16[4,96,1280]{2,1,0:T(8,128)(2,1)} %param.6) | copy-start | bytes 2949124
  40.2 0.7 %copy-start.2 = (s32[1,3]{1,0:T(1,128)S(1)}, s32[1,3]{1,0:T(1,128)}, u32[]{:S(2)}) copy-start(s32[1,3]{1,0:T(1,128)} %partner.1) | copy-start | bytes 40
  40.9 0.7 %copy-start.3 = (s32[1,3]{1,0:T(1,128)S(1)}, s32[1,3]{1,0:T(1,128)}, u32[]{:S(2)}) copy-start(s32[1,3]{1,0:T(1,128)} %counts.1) | copy-start | bytes 40
  41.5 0.9 %copy-start.4 = (bf16[128,384]{1,0:T(8,128)(2,1)S(1)}, bf16[128,384]{1,0:T(8,128)(2,1)}, u32[]{:S(2)}) copy-start(bf16[128,384]{1,0:T(8,128)(2,1)} %constant.14.t2) | copy-start | bytes 294916
  42.4 0.9 %copy-start.5 = (bf16[128,384]{1,0:T(8,128)(2,1)S(1)}, bf16[128,384]{1,0:T(8,128)(2,1)}, u32[]{:S(2)}) copy-start(bf16[128,384]{1,0:T(8,128)(2,1)} %constant.13.t1) | copy-start | bytes 294916

commit v3 on v2

--- a/solution.py
+++ b/solution.py
@@ -148,7 +148,8 @@
             pltpu.SemaphoreType.DMA((2,)),
             pltpu.SemaphoreType.DMA((2,)),
         ],
-        compiler_params=pltpu.CompilerParams(collective_id=0, has_side_effects=True, vmem_limit_bytes=24 * 2**20),
+        compiler_params=pltpu.CompilerParams(collective_id=0, has_side_effects=True, vmem_limit_bytes=25000000),
+        cost_estimate=pl.CostEstimate(flops=20_000_000_000, bytes_accessed=4_000_000, transcendentals=0),
         name="white_blocks",
     )(raw_samples.reshape(segments * local, channels), forward_table().reshape(n, local, WIDTH))
 
@@ -180,11 +181,11 @@
         count = jnp.full((8, LAGS), counts[0, slot].astype(jnp.float32), jnp.float32)
         scales.append((lax.rsqrt(count) * (live * (1.0 / math.sqrt(BINS))))[0:1])
 
-    def fill(pair):
+    def fill(pair, base):
         w = buffers[pair % 2]
         for s in range(segments):
-            x8 = rows[s, pl.ds(first, ROWS_PER_STEP), :]
-            y8 = swapped[s, pl.ds(first, ROWS_PER_STEP), :]
+            x8 = rows[s, pl.ds(base, ROWS_PER_STEP), :]
+            y8 = swapped[s, pl.ds(base, ROWS_PER_STEP), :]
             for k in range(2):
                 i = 2 * pair + k
                 x = jnp.broadcast_to(x8[i:i + 1], (16, width)).astype(jnp.bfloat16)
@@ -194,10 +195,17 @@
                         x * t1[m:m + 16, :] + y * t2[m:m + 16, :])
 
     pairs = ROWS_PER_STEP // 2
-    fill(0)
+    later = pl.multiple_of(jnp.minimum(first + ROWS_PER_STEP, block - ROWS_PER_STEP), ROWS_PER_STEP)
+
+    @pl.when(step == 0)
+    def _():
+        fill(0, first)
+
     for pair in range(pairs):
         if pair + 1 < pairs:
-            fill(pair + 1)
+            fill(pair + 1, first)
+        else:
+            fill(0, later)
         result = lax.dot_general(right[...], buffers[pair % 2][...], (((1,), (1,)), ((), ())),
                                  preferred_element_type=jnp.float32)
         for k in range(2):
@@ -218,9 +226,9 @@
     return pl.pallas_call(
         correlate_kernel,
         grid_spec=pltpu.PrefetchScalarGridSpec(
-            num_scalar_prefetch=2,
+            num_scalar_prefetch=0,
             grid=(block // ROWS_PER_STEP,),
-            in_specs=[vmem] * 5,
+            in_specs=[pl.BlockSpec(memory_space=pltpu.SMEM)] * 2 + [vmem] * 5,
             out_specs=pl.BlockSpec((1, SLOTS, ROWS_PER_STEP, block, LAGS), lambda i, *_: (0, 0, i, 0, 0)),
             scratch_shapes=[
                 pltpu.VMEM((SLOTS * block, depth), jnp.bfloat16),

time: 58.5 us -> 55.5 us (0.949)
  local copies, waits for them, and re-layouts: 5.56 us -> 2.49 us
    unnamed x12, local copies, waits for them, and re-layouts: 5.56 us -> 2.49 us
where the time goes in v3:
time: 55.5 us; the launch traced here: 55.3 us
  Pallas kernels  52.8 us (95%)
  local copies, waits for them, and re-layouts  2.49 us (4%)
    pallas_call x1, Pallas kernels, white_blocks(): pl.pallas_call(functools.partial(spectra_kernel, n, segments), out_shape=...  37.9 us
    pallas_call x1, Pallas kernels, correlate(): pl.pallas_call(correlate_kernel, grid_spec=pltpu.PrefetchScalarGridSpec(n...  14.9 us
    unnamed x12, local copies, waits for them, and re-layouts  2.49 us

profile of v3, /device:TPU:24, one launch (start us, length us, event | category | flops | bytes accessed | tf_op | source)
XLA Modules:
  0.0 55.3 jit_solution(252740923009794052)
XLA Ops:
  0.0 0.0 copy-start
  0.0 1.2 %copy-done = bf16[4,96,1280]{2,1,0:T(8,128)(2,1)S(1)} copy-done((bf16[4,96,1280]{2,1,0:T(8,128)(2,1)S(1)}, bf16[4,96,1280]{2,1,0:T(8,128)(2,1)}, u32[]{:S(2)}) %copy-start) | copy-done | bytes 983064
  1.2 0.0 copy-start.3
  1.2 1.3 %copy-done.3 = bf16[16,96,384]{2,1,0:T(8,128)(2,1)S(1)} copy-done((bf16[16,96,384]{2,1,0:T(8,128)(2,1)S(1)}, bf16[16,96,384]{2,1,0:T(8,128)(2,1)}, u32[]{:S(2)}) %copy-start.3) | copy-done | bytes 1179672
  2.5 0.0 copy-start.1
  2.5 0.0 copy-start.2
  2.5 0.0 copy-start.4
  2.5 0.0 copy-start.5
  2.5 37.9 %white_blocks.1 = (bf16[4,80,384]{2,1,0:T(8,128)(2,1)S(1)}, bf16[4,80,384]{2,1,0:T(8,128)(2,1)S(1)}, bf16[4,80,384]{2,1,0:T(8,128)(2,1)S(1)}) custom-call(bf16[384,1280]{1,0:T(8,128)(2,1)S(1)} %bitcast.1, bf16[16,96,384]{2,1,0:T(8,128)(2,1)S(1)} %copy-done.3), custom_call_target="tpu_custom_call" | custom-call | flops 20000000000 | bytes 4000000 | tf_op jit(solution)/shard_map/white_blocks/pallas_call | solution.py:137
  40.4 0.0 copy-done.1
  40.4 0.0 copy-done.2
  40.4 0.0 copy-done.4
  40.4 0.0 copy-done.5
  40.4 14.9 %correlate.1 = bf16[1,3,80,80,128]{4,3,2,1,0:T(8,128)(2,1)} custom-call(s32[1,3]{1,0:T(1,128)S(1)} %copy-done.1, s32[1,3]{1,0:T(1,128)S(1)} %copy-done.2, bf16[4,80,384]{2,1,0:T(8,128)(2,1)S(1)} %get-tuple-element.8.own, bf16[4,80,384]{2,1,0:T(8,128)(2,1)S(1)} %get-tuple-element.9.near, bf16[4,80,384]{2,1,0:T(8,128)(2,1)S(1)} %get-tuple-element.10.far, ...), custom_call_target="tpu_custom_call" | custom-call | flops 7549747200 | bytes 6000000 | tf_op jit(solution)/shard_map/correlate/pallas_call | solution.py:226
Async XLA Ops:
  0.0 1.2 %copy-start = (bf16[4,96,1280]{2,1,0:T(8,128)(2,1)S(1)}, bf16[4,96,1280]{2,1,0:T(8,128)(2,1)}, u32[]{:S(2)}) copy-start(bf16[4,96,1280]{2,1,0:T(8,128)(2,1)} %param.6) | copy-start | bytes 2949124
  1.2 1.3 %copy-start.3 = (bf16[16,96,384]{2,1,0:T(8,128)(2,1)S(1)}, bf16[16,96,384]{2,1,0:T(8,128)(2,1)}, u32[]{:S(2)}) copy-start(bf16[16,96,384]{2,1,0:T(8,128)(2,1)} %constant.12.table) | copy-start | bytes 3538948
  2.5 37.9 %copy-start.1 = (s32[1,3]{1,0:T(1,128)S(1)}, s32[1,3]{1,0:T(1,128)}, u32[]{:S(2)}) copy-start(s32[1,3]{1,0:T(1,128)} %partner.1) | copy-start | bytes 40
  2.5 37.9 %copy-start.2 = (s32[1,3]{1,0:T(1,128)S(1)}, s32[1,3]{1,0:T(1,128)}, u32[]{:S(2)}) copy-start(s32[1,3]{1,0:T(1,128)} %counts.1) | copy-start | bytes 40
  2.5 37.9 %copy-start.4 = (bf16[128,384]{1,0:T(8,128)(2,1)S(1)}, bf16[128,384]{1,0:T(8,128)(2,1)}, u32[]{:S(2)}) copy-start(bf16[128,384]{1,0:T(8,128)(2,1)} %constant.14.t2) | copy-start | bytes 294916
  2.5 37.9 %copy-start.5 = (bf16[128,384]{1,0:T(8,128)(2,1)S(1)}, bf16[128,384]{1,0:T(8,128)(2,1)}, u32[]{:S(2)}) copy-start(bf16[128,384]{1,0:T(8,128)(2,1)} %constant.13.t1) | copy-start | bytes 294916

commit v4 on v3

--- a/solution.py
+++ b/solution.py
@@ -17,7 +17,7 @@
 SLOTS = 3
 WIDTH = 2 * BINS
 HALF = BINS - 128
-ROWS_PER_STEP = 8
+ROWS_PER_STEP = 16
 MESH = pl.DeviceIdType.MESH
 
 

time: 55.5 us -> 54.3 us (0.978)
  Pallas kernels: 52.8 us -> 51.6 us
    pallas_call x1, Pallas kernels: 14.9 us -> 13.7 us  [correlate(): pl.pallas_call(correlate_kernel, grid_spec=pltpu.PrefetchScalarGridSpec(n...]
where the time goes in v4:
time: 54.3 us; the launch traced here: 54.1 us
  Pallas kernels  51.6 us (95%)
  local copies, waits for them, and re-layouts  2.49 us (5%)
    pallas_call x1, Pallas kernels, white_blocks(): pl.pallas_call(functools.partial(spectra_kernel, n, segments), out_shape=...  37.9 us
    pallas_call x1, Pallas kernels, correlate(): pl.pallas_call(correlate_kernel, grid_spec=pltpu.PrefetchScalarGridSpec(n...  13.7 us
    unnamed x12, local copies, waits for them, and re-layouts  2.49 us

profile of v4, /device:TPU:24, one launch (start us, length us, event | category | flops | bytes accessed | tf_op | source)
XLA Modules:
  0.0 54.1 jit_solution(4800698359509024007)
XLA Ops:
  0.0 0.0 copy-start
  0.0 1.2 %copy-done = bf16[4,96,1280]{2,1,0:T(8,128)(2,1)S(1)} copy-done((bf16[4,96,1280]{2,1,0:T(8,128)(2,1)S(1)}, bf16[4,96,1280]{2,1,0:T(8,128)(2,1)}, u32[]{:S(2)}) %copy-start) | copy-done | bytes 983064
  1.2 0.0 copy-start.3
  1.2 1.3 %copy-done.3 = bf16[16,96,384]{2,1,0:T(8,128)(2,1)S(1)} copy-done((bf16[16,96,384]{2,1,0:T(8,128)(2,1)S(1)}, bf16[16,96,384]{2,1,0:T(8,128)(2,1)}, u32[]{:S(2)}) %copy-start.3) | copy-done | bytes 1179672
  2.5 0.0 copy-start.1
  2.5 0.0 copy-start.2
  2.5 0.0 copy-start.4
  2.5 0.0 copy-start.5
  2.5 37.9 %white_blocks.1 = (bf16[4,80,384]{2,1,0:T(8,128)(2,1)S(1)}, bf16[4,80,384]{2,1,0:T(8,128)(2,1)S(1)}, bf16[4,80,384]{2,1,0:T(8,128)(2,1)S(1)}) custom-call(bf16[384,1280]{1,0:T(8,128)(2,1)S(1)} %bitcast.1, bf16[16,96,384]{2,1,0:T(8,128)(2,1)S(1)} %copy-done.3), custom_call_target="tpu_custom_call" | custom-call | flops 20000000000 | bytes 4000000 | tf_op jit(solution)/shard_map/white_blocks/pallas_call | solution.py:137
  40.4 0.0 copy-done.1
  40.4 0.0 copy-done.2
  40.4 0.0 copy-done.4
  40.4 0.0 copy-done.5
  40.4 13.7 %correlate.1 = bf16[1,3,80,80,128]{4,3,2,1,0:T(8,128)(2,1)} custom-call(s32[1,3]{1,0:T(1,128)S(1)} %copy-done.1, s32[1,3]{1,0:T(1,128)S(1)} %copy-done.2, bf16[4,80,384]{2,1,0:T(8,128)(2,1)S(1)} %get-tuple-element.8.own, bf16[4,80,384]{2,1,0:T(8,128)(2,1)S(1)} %get-tuple-element.9.near, bf16[4,80,384]{2,1,0:T(8,128)(2,1)S(1)} %get-tuple-element.10.far, ...), custom_call_target="tpu_custom_call" | custom-call | flops 7549747200 | bytes 6000000 | tf_op jit(solution)/shard_map/correlate/pallas_call | solution.py:226
Async XLA Ops:
  0.0 1.2 %copy-start = (bf16[4,96,1280]{2,1,0:T(8,128)(2,1)S(1)}, bf16[4,96,1280]{2,1,0:T(8,128)(2,1)}, u32[]{:S(2)}) copy-start(bf16[4,96,1280]{2,1,0:T(8,128)(2,1)} %param.6) | copy-start | bytes 2949124
  1.2 1.3 %copy-start.3 = (bf16[16,96,384]{2,1,0:T(8,128)(2,1)S(1)}, bf16[16,96,384]{2,1,0:T(8,128)(2,1)}, u32[]{:S(2)}) copy-start(bf16[16,96,384]{2,1,0:T(8,128)(2,1)} %constant.12.table) | copy-start | bytes 3538948
  2.5 37.9 %copy-start.1 = (s32[1,3]{1,0:T(1,128)S(1)}, s32[1,3]{1,0:T(1,128)}, u32[]{:S(2)}) copy-start(s32[1,3]{1,0:T(1,128)} %partner.1) | copy-start | bytes 40
  2.5 37.9 %copy-start.2 = (s32[1,3]{1,0:T(1,128)S(1)}, s32[1,3]{1,0:T(1,128)}, u32[]{:S(2)}) copy-start(s32[1,3]{1,0:T(1,128)} %counts.1) | copy-start | bytes 40
  2.5 37.9 %copy-start.4 = (bf16[128,384]{1,0:T(8,128)(2,1)S(1)}, bf16[128,384]{1,0:T(8,128)(2,1)}, u32[]{:S(2)}) copy-start(bf16[128,384]{1,0:T(8,128)(2,1)} %constant.14.t2) | copy-start | bytes 294916
  2.5 37.9 %copy-start.5 = (bf16[128,384]{1,0:T(8,128)(2,1)S(1)}, bf16[128,384]{1,0:T(8,128)(2,1)}, u32[]{:S(2)}) copy-start(bf16[128,384]{1,0:T(8,128)(2,1)} %constant.13.t1) | copy-start | bytes 294916
